TPU v7x, 32 devices: a whole 2x2x4 slice. The times are simulated.
32 devices in a mesh: aa: 4 (over x, core), ba: 8 (over z, y).
Axes of the slice: x: 2, y: 2, z: 4, core: 2. Of those that a mesh axis runs over, the one named last changes fastest.
Arguments:
- head_outputs: bfloat16 [1024, 4096], P('ba'), may hold values from -6 to 6
- stream: bfloat16 [1024, 4096], P('ba'), may hold values from -6 to 6
- adapter_down_factors: bfloat16 [4096, 512], P(None, 'aa'), may hold values from -0.09375 to 0.09375
- adapter_up_factors: bfloat16 [512, 4096], P('aa'), may hold values from -1.5 to 1.5
- norm_gain_vector: float32 [4096], replicated, may hold values from 0.5 to 1.5
- router_matrix: bfloat16 [4096, 8], replicated, may hold values from -0.09375 to 0.09375
- token_adapter_index: int32 [1024], P('ba'), may hold values from 0 to 31
- token_expert_index: int32 [1024, 2], P('ba'), may hold values from 0 to 7, all different within a row; in each aligned block of 128 rows (0 to 127, 128 to 255, ...) at most 48 rows name the same one
- gate_weight: bfloat16 [8, 4096, 14336], P('ba', None, 'aa'), may hold values from -0.09375 to 0.09375
- up_weight: bfloat16 [8, 4096, 14336], P('ba', None, 'aa'), may hold values from -0.09375 to 0.09375
- down_weight: bfloat16 [8, 14336, 4096], P('ba', 'aa'), may hold values from -0.046875 to 0.046875
Outputs:
- mixed: bfloat16 [1024, 4096], P('ba', 'aa')
- adapter_load: float32 [32], P('aa')
Inputs may be any that keep to these rules, and one draw needn't show every extreme that they name: `token_expert_index`: the two experts of a row differ; in each aligned block of 128 rows no expert is named by more than 48 rows.
All inputs are finite; a program needn't handle non-finite values.
Results may differ from a plain program's by a relative error of at most 0.0049.
Values may be sent and summed in bfloat16 or wider, within the bound.
A program may use at most 192 MiB of HBM per device.

v0:
```python
import jax
import jax.numpy as jnp
from jax import lax
from jax.sharding import PartitionSpec as P

E = 8
ADAPTER_RANK = 16
CAP = 48


EPS = 1e-05
ADAPTER_SCALE = 2.0


def shards(
    head_outputs,
    stream,
    adapter_down_factors,
    adapter_up_factors,
    norm_gain_vector,
    router_matrix,
    token_adapter_index,
    token_expert_index,
    gate_weight,
    up_weight,
    down_weight,
):
    tok_rows = head_outputs.shape[0]
    model_width = head_outputs.shape[1]
    held_count = adapter_down_factors.shape[1] // ADAPTER_RANK
    groups = lax.axis_size("aa")
    index_aa = lax.axis_index("aa")
    local_ids = token_adapter_index - index_aa * held_count
    column_holder = jnp.arange(adapter_down_factors.shape[1], dtype=jnp.int32) // ADAPTER_RANK
    rank_projected = jnp.dot(head_outputs, adapter_down_factors, preferred_element_type=jnp.float32)
    rank_projected = jnp.where(
        local_ids[:, None] == column_holder[None, :], rank_projected, 0.0
    ).astype(jnp.bfloat16)
    partial_update = ADAPTER_SCALE * jnp.dot(
        rank_projected, adapter_up_factors, preferred_element_type=jnp.float32
    )
    tallies = jnp.sum(
        (local_ids[:, None] == jnp.arange(held_count, dtype=jnp.int32)[None, :]).astype(
            jnp.float32
        ),
        axis=0,
    )
    adapter_load = lax.psum(tallies, "ba")
    share_width = model_width // groups
    adapter_update = lax.psum(partial_update, "aa")
    residual_stream = stream.astype(jnp.float32) + adapter_update
    inv_norm = lax.rsqrt(jnp.mean(residual_stream * residual_stream, axis=1, keepdims=True) + EPS)
    normed = (residual_stream * inv_norm * norm_gain_vector).astype(jnp.bfloat16)
    residual_share = lax.dynamic_slice_in_dim(
        residual_stream, index_aa * share_width, share_width, 1
    )
    logits = jnp.dot(normed, router_matrix, preferred_element_type=jnp.float32)
    experts_iota = jnp.arange(E, dtype=jnp.int32)
    chosen = (token_expert_index[:, :, None] == experts_iota[None, None, :]).astype(jnp.float32)
    picked = jnp.sum(chosen * logits[:, None, :], axis=2)
    weights = 1.0 / (1.0 + jnp.exp(picked[:, ::-1] - picked))
    flat_experts = token_expert_index.reshape(-1)
    expert_hits = (flat_experts[:, None] == experts_iota[None, :]).astype(jnp.int32)
    before = jnp.cumsum(expert_hits, axis=0) - expert_hits
    slot_index = flat_experts * CAP + jnp.sum(before * expert_hits, axis=1)
    slots_iota = jnp.arange(E * CAP, dtype=jnp.int32)
    placed = slot_index[None, :] == slots_iota[:, None]
    pick_rows = jnp.sum(placed.astype(jnp.float32).reshape(E * CAP, tok_rows, 2), axis=2).astype(
        jnp.bfloat16
    )
    outgoing = jnp.dot(pick_rows, normed, preferred_element_type=jnp.float32).astype(jnp.bfloat16)
    halves = lax.axis_size("ba") // E
    outgoing = jnp.repeat(outgoing.reshape(E, CAP, model_width), halves, axis=0)
    mixing = jnp.where(placed, weights.reshape(1, -1), 0.0)
    mixing = jnp.sum(mixing.reshape(E * CAP, tok_rows, 2), axis=2)
    received = lax.all_to_all(outgoing, "ba", split_axis=0, concat_axis=0, tiled=True)
    sources = received.shape[0]
    items = received.shape[1]
    flat_rows = received.reshape(sources * items, model_width)
    gate_proj = jnp.dot(flat_rows, gate_weight[0], preferred_element_type=jnp.float32)
    up_proj = jnp.dot(flat_rows, up_weight[0], preferred_element_type=jnp.float32)
    hidden = (jax.nn.silu(gate_proj) * up_proj).astype(jnp.bfloat16)
    partial_value = jnp.dot(hidden, down_weight[0], preferred_element_type=jnp.float32).reshape(
        sources, items, model_width
    )
    reduced = lax.psum_scatter(partial_value, "aa", scatter_dimension=2, tiled=True)
    returned = lax.all_to_all(reduced, "ba", split_axis=0, concat_axis=0, tiled=True)
    summed = jnp.sum(returned.reshape(E, halves, CAP, returned.shape[2]), axis=1).reshape(
        E * CAP, returned.shape[2]
    )
    gathered = jnp.einsum("sr,sd->rd", mixing, summed, precision=lax.Precision.HIGHEST)
    mixed_share = residual_share + gathered
    return (mixed_share.astype(jnp.bfloat16), adapter_load)


def solution(mesh):
    in_specs = (
        P("ba", None),
        P("ba", None),
        P(None, "aa"),
        P("aa", None),
        P(),
        P(),
        P("ba"),
        P("ba", None),
        P("ba", None, "aa"),
        P("ba", None, "aa"),
        P("ba", "aa", None),
    )
    out_specs = (P("ba", "aa"), P("aa"))
    return jax.shard_map(shards, mesh=mesh, in_specs=in_specs, out_specs=out_specs, check_vma=False)
```

profile of v0, /device:TPU:8, one launch (start us, length us, event | category | flops | bytes accessed | tf_op | source)
XLA Modules:
  0.0 317.9 jit_solution(642658996399779848)
XLA Ops:
  7.2 0.0 copy-start
  7.2 0.0 all-reduce.2.cloned.1.call-start
  7.2 0.7 and_select_fusion
  8.0 0.4 copy-done
  8.4 3.6 %convolution_multiply_fusion = f32[128,4096]{1,0:T(8,128)} fusion(bf16[128,4096]{1,0:T(8,128)(2,1)S(1)} %copy-done, bf16[128,4096]{1,0:T(8,128)(2,1)} %param.11, bf16[4096,128]{1,0:T(8,128)(2,1)} %param.13, s32[128]{0:T(128)S(1)} %get-tuple-element.6, s32[128]{0:T(128)S(1)} %get-tuple-element.7), kind=kOutput, calls=%fused_computation.9 | convolution fusion | flops 269008896 | bytes 5243904 | tf_op jit(solution)/shard_map/dot_general | solution.py:39
  12.1 0.0 all-reduce.2.cloned.1.call-update
  12.1 0.0 copy-start.3
  12.1 0.0 copy-start.4
  12.1 0.0 reduce-scatter.2.cloned.1.call-start
  12.2 0.1 copy.27
  12.3 0.1 eq.86
  12.4 0.1 eq.82
  12.6 0.6 reduce-window.6
  13.2 0.2 slice_reduce_fusion
  13.4 0.1 fusion.20
  13.5 0.1 reduce_sum.61
  13.7 0.1 copy.29
  13.7 51.0 %all-reduce.2.cloned.1.call-done = f32[128,4096]{1,0:T(8,128)} async-done(((f32[128,4096]{1,0:T(8,128)}), f32[128,4096]{1,0:T(8,128)}) %all-reduce.2.cloned.1.call-update) | async-done | bytes 2097168 | tf_op jit(solution)/shard_map/psum | solution.py:50
  64.8 2.0 multiply_reduce_fusion
  66.8 0.4 fusion.23
  67.3 0.1 convert_reduce_fusion
  67.4 1.0 convolution_convert_fusion
  68.5 75.4 %all_to_all.10 = bf16[8,48,4096]{2,1,0:T(8,128)(2,1)S(1)} all-to-all(bf16[8,48,4096]{2,1,0:T(8,128)(2,1)S(1)} %bitcast.36), channel_id=1, replica_groups=mesh['aa'=4,'ba'=8] {'ba'}, dimensions={0} | all-to-all | bytes 6291456 | tf_op jit(solution)/shard_map/all_to_all | solution.py:76
  143.9 17.6 %fusion.4 = f32[384,3584]{1,0:T(8,128)} fusion(bf16[384,4096]{1,0:T(8,128)(2,1)S(1)} %bitcast.37, bf16[1,4096,3584]{2,1,0:T(8,128)(2,1)} %param.19), kind=kOutput, calls=%fused_computation.4 | convolution fusion | flops 11274289152 | bytes 38010880 | tf_op jit(solution)/shard_map/dot_general | solution.py:80
  161.5 19.0 %fusion.9 = bf16[384,3584]{1,0:T(8,128)(2,1)} fusion(bf16[384,4096]{1,0:T(8,128)(2,1)S(1)} %bitcast.38, bf16[1,4096,3584]{2,1,0:T(8,128)(2,1)} %param.20, f32[384,3584]{1,0:T(8,128)} %fusion.4), kind=kOutput, calls=%fused_computation.7 | convolution fusion | flops 11282546688 | bytes 40763392 | tf_op jit(solution)/shard_map/dot_general | solution.py:81
  180.5 19.3 %fusion = f32[8,48,4096]{2,1,0:T(8,128)} fusion(bf16[8,48,3584]{2,1,0:T(8,128)(2,1)} %bitcast.39, bf16[1,3584,4096]{2,1,0:T(8,128)(2,1)} %param.21), kind=kOutput, calls=%fused_computation | convolution fusion | flops 11274289152 | bytes 38404096 | tf_op jit(solution)/shard_map/dot_general | solution.py:83
  199.8 0.0 reduce-scatter.2.cloned.1.call-update
  199.9 56.7 %reduce-scatter.2.cloned.1.call-done = f32[8,48,1024]{2,1,0:T(8,128)} async-done(((f32[8,48,4096]{2,1,0:T(8,128)}), f32[8,48,1024]{2,1,0:T(8,128)}) %reduce-scatter.2.cloned.1.call-update) | async-done | bytes 1572880 | tf_op jit(solution)/shard_map/reduce_scatter | solution.py:86
  256.6 6.0 %all-to-all-start.1 = ((f32[8,48,1024]{2,1,0:T(8,128)}), f32[8,48,1024]{2,1,0:T(8,128)}, u32[]{:S(2)}, u32[]{:S(2)}) async-start(f32[8,48,1024]{2,1,0:T(8,128)} %reduce-scatter.2.cloned.1.call-done), calls=%async_computation.2 | async-start | bytes 3145728 | tf_op jit(solution)/shard_map/all_to_all | solution.py:87
  262.6 0.1 convert_reduce_fusion.1
  262.8 45.0 %psum.15 = f32[8]{0:T(128)} all-reduce(f32[8]{0:T(128)S(1)} %convert_reduce_fusion.1), channel_id=1, replica_groups=mesh['aa'=4,'ba'=8] {'ba'}, use_global_device_ids=true, to_apply=%region_10.11 | all-reduce | flops 8 | bytes 64 | tf_op jit(solution)/shard_map/psum | solution.py:48
  307.8 3.2 %fusion.12 = bf16[128,1024]{1,0:T(8,128)(2,1)} fusion(f32[384,128]{1,0:T(8,128)S(1)} %get-tuple-element.3, f32[384,1024]{1,0:T(8,128)} %bitcast.9, f32[128,4096]{1,0:T(8,128)S(1)} %get-tuple-element.5, s32[]{:T(128)S(6)} %select_n.23), kind=kOutput, calls=%fused_computation.14 | convolution fusion | flops 604241920 | bytes 2555908 | tf_op jit(solution)/shard_map/sr,sd->rd/dot_general | solution.py:91
  (17 shorter events, 0.1 us)
Async XLA Ops:
  7.2 1.2 copy-start
  7.2 57.6 %all-reduce.2.cloned.1.call-start = ((), (), s32[]{:S(2)}) async-start(), calls=%async_computation.3 | async-start | bytes 4194304 | tf_op jit(solution)/shard_map/psum | solution.py:50
  8.4 3.7 %copy-start.5 = (s32[128,2]{0,1:T(2,128)S(1)}, s32[128,2]{0,1:T(2,128)}, u32[]{:S(2)}) copy-start(s32[128,2]{0,1:T(2,128)} %param.18) | copy-start | bytes 3076
  12.1 52.7 %copy-start.2 = (bf16[128,4096]{1,0:T(8,128)(2,1)S(1)}, bf16[128,4096]{1,0:T(8,128)(2,1)}, u32[]{:S(2)}) copy-start(bf16[128,4096]{1,0:T(8,128)(2,1)} %param.12) | copy-start | bytes 3145732
  12.1 54.7 %copy-start.3 = (f32[4096]{0:T(1024)S(1)}, f32[4096]{0:T(1024)}, u32[]{:S(2)}) copy-start(f32[4096]{0:T(1024)} %param.15) | copy-start | bytes 49156
  12.1 54.7 %copy-start.4 = (bf16[4096,8]{0,1:T(8,128)(2,1)S(1)}, bf16[4096,8]{0,1:T(8,128)(2,1)}, u32[]{:S(2)}) copy-start(bf16[4096,8]{0,1:T(8,128)(2,1)} %param.16) | copy-start | bytes 196612
  12.1 244.5 %reduce-scatter.2.cloned.1.call-start = ((), (), s32[]{:S(2)}) async-start(), calls=%async_computation.4 | async-start | bytes 7864320 | tf_op jit(solution)/shard_map/reduce_scatter | solution.py:86
  199.9 111.2 %copy-start.1 = (bf16[128,4096]{1,0:T(8,128)(2,1)S(1)}, bf16[128,4096]{1,0:T(8,128)(2,1)}, u32[]{:S(2)}) copy-start(bf16[128,4096]{1,0:T(8,128)(2,1)} %param.14) | copy-start | bytes 3145732
  256.6 51.2 %all-to-all-start.1 = ((f32[8,48,1024]{2,1,0:T(8,128)}), f32[8,48,1024]{2,1,0:T(8,128)}, u32[]{:S(2)}, u32[]{:S(2)}) async-start(f32[8,48,1024]{2,1,0:T(8,128)} %reduce-scatter.2.cloned.1.call-done), calls=%async_computation.2 | async-start | bytes 3145728 | tf_op jit(solution)/shard_map/all_to_all | solution.py:87
Sparse Core Ops, SparseCore 0:
  12.2 52.5 all-reduce.1
  200.0 56.5 reduce-scatter.1
where the time goes:
time: 318 us
  blocking collectives  120 us (38%)
  waiting for transfers between devices  108 us (34%)
  matrix products  64.3 us (20%)
  between operations  14.2 us (4%)
  starting transfers between devices  6.13 us (2%)
  other arithmetic  3.7 us (1%)
    all_to_all x1, blocking collectives, shards(): lax.all_to_all(outgoing, 'ba', split_axis=0, concat_axis=0, tiled=True)  75.4 us
    reduce_scatter x1, waiting for transfers between devices, shards(): lax.psum_scatter(partial_value, 'aa', scatter_dimension=2, tiled=True)  56.7 us
    psum x1, waiting for transfers between devices, shards(): adapter_update = lax.psum(partial_update, 'aa')  51 us
    psum x1, blocking collectives, shards(): adapter_load = lax.psum(tallies, 'ba')  45 us
    dot_general x1, matrix products, shards(): jnp.dot(hidden, down_weight[0], preferred_element_type=jnp.float32)  19.3 us
    dot_general x1, matrix products, shards(): jnp.dot(flat_rows, up_weight[0], preferred_element_type=jnp.float32)  19 us
    dot_general x1, matrix products, shards(): jnp.dot(flat_rows, gate_weight[0], preferred_element_type=jnp.float32)  17.6 us
  transfers between devices with their start and end apart: 3, of which 2 were waited for; matrix products, arithmetic and copies ran while one was open for 1% of the time, Pallas kernels for 0%

commit v1 on v0

v1 whole, which is shorter than its diff:
```python
import functools

import jax
import jax.numpy as jnp
from jax import lax
from jax.experimental import pallas as pl
from jax.experimental.pallas import tpu as pltpu
from jax.sharding import PartitionSpec as P

E = 8
ADAPTER_RANK = 16
CAP = 48
CORES = 2

EPS = 1e-05
ADAPTER_SCALE = 2.0
MESH = pl.DeviceIdType.MESH
F32 = jnp.float32
BF16 = jnp.bfloat16


def cols(block, width):
    return pl.ds(pl.multiple_of(block * width, 128), width)


def greet(places):
    barrier = pltpu.get_barrier_semaphore()
    for place in places:
        pl.semaphore_signal(barrier, inc=1, device_id=place, device_id_type=MESH)
    pl.semaphore_wait(barrier, len(places))


def send(src, dst, send_sem, recv_sem, place):
    copy = pltpu.make_async_remote_copy(
        src_ref=src,
        dst_ref=dst,
        send_sem=send_sem,
        recv_sem=recv_sem,
        device_id=place,
        device_id_type=MESH,
    )
    copy.start()
    return copy


def peers(axis, me, n):
    return [{axis: lax.rem(me + k, n)} for k in range(1, n)]


def front(
    n_aa, n_ba, model_width,
    idx_ref, idxt_ref, head_ref, stream_ref, down_ref, gain_ref, router_ref, up_ref,
    x_ref, res_ref, logit_ref, load_ref,
    up_all, low_all, sq_all, lg_all, ld_all, outgoing,
    own_sem, up_s, up_r, low_s, low_r, sq_s, sq_r, lg_s, lg_r, ld_s, ld_r,
    ba_s, ba_r, xg_s, xg_r, cg_s, cg_r,
):
    aa, ba = lax.axis_index("aa"), lax.axis_index("ba")
    nx = n_aa // CORES
    x, core = aa // CORES, lax.rem(aa, CORES)
    partner = {"aa": x * CORES + 1 - core}
    toks = head_ref.shape[0]
    held = down_ref.shape[1]
    width = model_width // n_aa
    halves = n_ba // E
    aa_peers, ba_peers = peers("aa", aa, n_aa), peers("ba", ba, n_ba)
    greet(aa_peers + ba_peers)
    pending = []

    def fan(places, src, dst, s, r):
        copies = [send(src, dst, s.at[i], r.at[i], p) for i, p in enumerate(places)]
        pending.extend(copies)
        return copies

    up_copies = []
    for k in range(1, n_aa):
        to = lax.rem(aa + k, n_aa)
        up_copies.append(send(
            up_ref.at[:, cols(to, width)], up_all.at[aa], up_s.at[k - 1], up_r.at[k - 1], {"aa": to}
        ))
    pending.extend(up_copies)
    own_up = pltpu.make_async_copy(up_ref.at[:, cols(aa, width)], up_all.at[aa], own_sem)
    own_up.start()

    local = idx_ref[:, 2:3] - aa * (held // ADAPTER_RANK)
    lanes = lax.broadcasted_iota(jnp.int32, (toks, held), 1)
    projected = jnp.dot(head_ref[...], down_ref[...], preferred_element_type=F32)
    low_all[aa] = jnp.where(local == lanes // ADAPTER_RANK, projected, 0.0).astype(BF16)
    low_copies = fan(aa_peers, low_all.at[aa], low_all.at[aa], low_s, low_r)

    tally = jnp.sum((local == lanes).astype(F32), axis=0, keepdims=True)
    ld_all[ba] = jnp.broadcast_to(tally, ld_all.shape[1:])
    ld_copies = fan(ba_peers, ld_all.at[ba], ld_all.at[ba], ld_s, ld_r)

    experts = lax.broadcasted_iota(jnp.int32, (E, toks), 0)
    hits = ((idxt_ref[0:1, :] == experts) | (idxt_ref[1:2, :] == experts)).astype(F32)
    earlier = (
        lax.broadcasted_iota(jnp.int32, (toks, toks), 0)
        < lax.broadcasted_iota(jnp.int32, (toks, toks), 1)
    ).astype(F32)
    place = jnp.dot(hits.astype(BF16), earlier.astype(BF16), preferred_element_type=F32)
    place = jnp.where(hits > 0.0, place, -1.0).astype(jnp.int32)
    spots = lax.broadcasted_iota(jnp.int32, (CAP, toks), 0)

    own_up.wait()
    for copy in low_copies + up_copies:
        copy.wait_recv()
    delta = jnp.dot(low_all[0], up_all[0], preferred_element_type=F32)
    for j in range(1, n_aa):
        delta = delta + jnp.dot(low_all[j], up_all[j], preferred_element_type=F32)
    residual = stream_ref[:, cols(aa, width)].astype(F32) + ADAPTER_SCALE * delta
    res_ref[...] = residual
    square = jnp.sum(residual * residual, axis=1, keepdims=True)
    sq_all[aa] = jnp.broadcast_to(square, sq_all.shape[1:])
    for copy in fan(aa_peers, sq_all.at[aa], sq_all.at[aa], sq_s, sq_r):
        copy.wait_recv()
    total = sq_all[0]
    for j in range(1, n_aa):
        total = total + sq_all[j]
    inv_norm = lax.rsqrt(total[:, 0:1] / model_width + EPS)
    normed = (res_ref[...] * inv_norm * gain_ref[:, cols(aa, width)]).astype(BF16)

    for e in range(E):
        pick = (place[e : e + 1, :] == spots).astype(F32).astype(BF16)
        rows = jnp.dot(pick, normed, preferred_element_type=F32).astype(BF16)
        for j in range(halves):
            outgoing[e * halves + j] = rows
    mine = cols(aa, width)
    ba_copies = []
    for k in range(1, n_ba):
        to = lax.rem(ba + k, n_ba)
        ba_copies.append(send(
            outgoing.at[to], x_ref.at[ba, :, mine], ba_s.at[k - 1], ba_r.at[k - 1], {"ba": to}
        ))
    pending.extend(ba_copies)
    x_ref[ba, :, mine] = outgoing[ba]

    part = jnp.dot(
        normed,
        router_ref[pl.ds(pl.multiple_of(aa * width, 128), width), :],
        preferred_element_type=F32,
    )
    lg_all[aa] = part
    lg_copies = fan(aa_peers, lg_all.at[aa], lg_all.at[aa], lg_s, lg_r)

    x_copies, c_copies = [], []
    for k in range(n_ba):
        source = lax.rem(ba - k + n_ba, n_ba)
        if k:
            ba_copies[k - 1].wait_recv()
        block = x_ref.at[source, :, mine]
        for kx in range(1, nx):
            to = lax.rem(x + kx, nx) * CORES + core
            i = k * (nx - 1) + kx - 1
            x_copies.append(send(block, block, xg_s.at[i], xg_r.at[i], {"aa": to}))
        c_copies.append(send(block, block, cg_s.at[k * nx], cg_r.at[k * nx], partner))
    for k in range(n_ba):
        source = lax.rem(ba - k + n_ba, n_ba)
        for kx in range(1, nx):
            x_copies[k * (nx - 1) + kx - 1].wait_recv()
            origin = lax.rem(x - kx + nx, nx) * CORES + core
            block = x_ref.at[source, :, cols(origin, width)]
            i = k * nx + kx
            c_copies.append(send(block, block, cg_s.at[i], cg_r.at[i], partner))
    pending.extend(x_copies + c_copies)

    for copy in lg_copies + ld_copies:
        copy.wait_recv()
    logits = lg_all[0]
    for j in range(1, n_aa):
        logits = logits + lg_all[j]
    logit_ref[...] = logits
    load = ld_all[0]
    for j in range(1, n_ba):
        load = load + ld_all[j]
    load_ref[...] = load
    for copy in c_copies:
        copy.wait_recv()
    for copy in pending:
        copy.wait_send()


def back(
    n_aa, n_ba,
    idx_ref, res_ref, logit_ref, y_ref,
    out_ref,
    c1, xs, c2, acc, bs, ret,
    c_s, c_r, x_s, x_r, b_s, b_r,
):
    aa, ba = lax.axis_index("aa"), lax.axis_index("ba")
    nx = n_aa // CORES
    x, core = aa // CORES, lax.rem(aa, CORES)
    partner = {"aa": x * CORES + 1 - core}
    toks, width = out_ref.shape
    halves = n_ba // E
    x_peers = [{"aa": lax.rem(x + kx, nx) * CORES + core} for kx in range(1, nx)]
    greet([partner] + x_peers + peers("ba", ba, n_ba))
    order = list(range(1, n_ba)) + [0]
    far_first = list(range(1, nx)) + [0]

    c_copies, x_copies, b_copies = {}, {}, {}
    for k in order:
        to = lax.rem(ba + k, n_ba)
        for kx in far_first:
            block = lax.rem(x + kx, nx) * CORES + 1 - core
            i = k * nx + kx
            c_copies[k, kx] = send(
                y_ref.at[to, :, cols(block, width)], c1.at[kx, k], c_s.at[i], c_r.at[i], partner
            )

    first, second = idx_ref[:, 0:1], idx_ref[:, 1:2]
    experts = lax.broadcasted_iota(jnp.int32, (toks, E), 1)
    hit0, hit1 = (first == experts).astype(F32), (second == experts).astype(F32)
    logits = logit_ref[...]
    own0 = jnp.sum(hit0 * logits, axis=1, keepdims=True)
    own1 = jnp.sum(hit1 * logits, axis=1, keepdims=True)
    weight0 = 1.0 / (1.0 + jnp.exp(own1 - own0))
    weight1 = 1.0 / (1.0 + jnp.exp(own0 - own1))
    earlier = (
        lax.broadcasted_iota(jnp.int32, (toks, toks), 1)
        < lax.broadcasted_iota(jnp.int32, (toks, toks), 0)
    ).astype(F32)
    place = jnp.dot(earlier.astype(BF16), (hit0 + hit1).astype(BF16), preferred_element_type=F32)
    spots = lax.broadcasted_iota(jnp.int32, (toks, n_ba * CAP), 1)

    def picked(expert, hit):
        spot = jnp.sum(hit * place, axis=1, keepdims=True).astype(jnp.int32)
        found = spots == expert * (halves * CAP) + spot
        for j in range(1, halves):
            found = found | (spots == (expert * halves + j) * CAP + spot)
        return found.astype(F32).astype(BF16)

    pick0, pick1 = picked(first, hit0), picked(second, hit1)

    for k in order:
        to = lax.rem(ba + k, n_ba)
        for kx in far_first:
            block = lax.rem(x + kx, nx) * CORES + core
            c_copies[k, kx].wait_recv()
            pair = y_ref[to, :, cols(block, width)].astype(F32) + c1[kx, k].astype(F32)
            if kx:
                i = k * (nx - 1) + kx - 1
                xs[kx - 1, k] = pair.astype(BF16)
                x_copies[k, kx] = send(
                    xs.at[kx - 1, k], c2.at[kx - 1, k], x_s.at[i], x_r.at[i], x_peers[kx - 1]
                )
            else:
                acc[k] = pair
    for k in order:
        total = acc[k]
        for kx in range(1, nx):
            x_copies[k, kx].wait_recv()
            total = total + c2[kx - 1, k].astype(F32)
        if k:
            bs[k - 1] = total.astype(BF16)
            b_copies[k] = send(
                bs.at[k - 1], ret.at[ba], b_s.at[k - 1], b_r.at[k - 1],
                {"ba": lax.rem(ba + k, n_ba)},
            )
        else:
            ret[ba] = total.astype(BF16)
    for k in range(1, n_ba):
        b_copies[k].wait_recv()
    rows = ret[...].reshape(n_ba * CAP, width)
    mixed = weight0 * jnp.dot(pick0, rows, preferred_element_type=F32)
    mixed = mixed + weight1 * jnp.dot(pick1, rows, preferred_element_type=F32)
    out_ref[...] = (res_ref[...] + mixed).astype(BF16)
    for copies in (c_copies, x_copies, b_copies):
        for copy in copies.values():
            copy.wait_send()


def shards(
    head_outputs,
    stream,
    adapter_down_factors,
    adapter_up_factors,
    norm_gain_vector,
    router_matrix,
    token_adapter_index,
    token_expert_index,
    gate_weight,
    up_weight,
    down_weight,
):
    toks, model_width = head_outputs.shape
    n_aa, n_ba = lax.axis_size("aa"), lax.axis_size("ba")
    nx = n_aa // CORES
    held = adapter_down_factors.shape[1]
    width = model_width // n_aa
    vmem = pl.BlockSpec(memory_space=pltpu.VMEM)
    dma = pltpu.SemaphoreType.DMA
    idx = jnp.concatenate([token_expert_index, token_adapter_index[:, None]], axis=1)

    def sems(n):
        return [dma((max(n, 1),)), dma((max(n, 1),))]

    x, residual, logits, load = pl.pallas_call(
        functools.partial(front, n_aa, n_ba, model_width),
        out_shape=(
            jax.ShapeDtypeStruct((n_ba, CAP, model_width), BF16),
            jax.ShapeDtypeStruct((toks, width), F32),
            jax.ShapeDtypeStruct((toks, E), F32),
            jax.ShapeDtypeStruct((8, held), F32),
        ),
        in_specs=[vmem] * 7 + [pl.BlockSpec(memory_space=pl.ANY)],
        out_specs=(vmem,) * 4,
        scratch_shapes=[
            pltpu.VMEM((n_aa, held, width), BF16),
            pltpu.VMEM((n_aa, toks, held), BF16),
            pltpu.VMEM((n_aa, toks, 128), F32),
            pltpu.VMEM((n_aa, toks, E), F32),
            pltpu.VMEM((n_ba, 8, held), F32),
            pltpu.VMEM((n_ba, CAP, width), BF16),
            dma,
        ]
        + sems(n_aa - 1) * 4
        + sems(n_ba - 1) * 2
        + sems(n_ba * (nx - 1))
        + sems(n_ba * nx),
        compiler_params=pltpu.CompilerParams(
            collective_id=0, has_side_effects=True, vmem_limit_bytes=48 * 2**20
        ),
        name="front",
    )(
        idx, token_expert_index.T, head_outputs, stream, adapter_down_factors,
        norm_gain_vector[None, :], router_matrix, adapter_up_factors,
    )
    rows = x.reshape(n_ba * CAP, model_width)
    gate_proj = jnp.dot(rows, gate_weight[0], preferred_element_type=F32)
    up_proj = jnp.dot(rows, up_weight[0], preferred_element_type=F32)
    hidden = (jax.nn.silu(gate_proj) * up_proj).astype(BF16)
    partial_value = jnp.dot(hidden, down_weight[0], preferred_element_type=F32).astype(BF16)
    mixed = pl.pallas_call(
        functools.partial(back, n_aa, n_ba),
        out_shape=jax.ShapeDtypeStruct((toks, width), BF16),
        in_specs=[vmem] * 4,
        out_specs=vmem,
        scratch_shapes=[
            pltpu.VMEM((nx, n_ba, CAP, width), BF16),
            pltpu.VMEM((max(nx - 1, 1), n_ba, CAP, width), BF16),
            pltpu.VMEM((max(nx - 1, 1), n_ba, CAP, width), BF16),
            pltpu.VMEM((n_ba, CAP, width), F32),
            pltpu.VMEM((n_ba - 1, CAP, width), BF16),
            pltpu.VMEM((n_ba, CAP, width), BF16),
        ]
        + sems(n_ba * nx)
        + sems(n_ba * (nx - 1))
        + sems(n_ba - 1),
        compiler_params=pltpu.CompilerParams(
            collective_id=1, has_side_effects=True, vmem_limit_bytes=56 * 2**20
        ),
        name="back",
    )(idx, residual, logits, partial_value.reshape(n_ba, CAP, model_width))
    return (mixed, load[0, : held // ADAPTER_RANK])


def solution(mesh):
    in_specs = (
        P("ba", None),
        P("ba", None),
        P(None, "aa"),
        P("aa", None),
        P(),
        P(),
        P("ba"),
        P("ba", None),
        P("ba", None, "aa"),
        P("ba", None, "aa"),
        P("ba", "aa", None),
    )
    out_specs = (P("ba", "aa"), P("aa"))
    return jax.shard_map(shards, mesh=mesh, in_specs=in_specs, out_specs=out_specs, check_vma=False)
```

time: 318 us -> 161 us (0.51)
  blocking collectives: 120 us -> 0 us
  waiting for transfers between devices: 108 us -> 0 us
  Pallas kernels: 0 us -> 86 us
  between operations: 14.2 us -> 0.69 us
  local copies, waits for them, and re-layouts: 1.31 us -> 11.4 us
  starting transfers between devices: 6.13 us -> 0 us
  matrix products: 64.3 us -> 59.8 us
    pallas_call x0 -> x2, Pallas kernels: none -> 86 us  [the longest x1 51.5 us: shards(): pl.pallas_call(functools.partial(front, n_aa, n_ba, model_width), out_sha...]
    all_to_all x1 -> x0, blocking collectives: 75.4 us -> none  [shards(): lax.all_to_all(outgoing, 'ba', split_axis=0, concat_axis=0, tiled=True)]
    reduce_scatter x1 -> x0, waiting for transfers between devices: 56.7 us -> none  [shards(): lax.psum_scatter(partial_value, 'aa', scatter_dimension=2, tiled=True)]
    psum x1 -> x0, waiting for transfers between devices: 51 us -> none  [shards(): adapter_update = lax.psum(partial_update, 'aa')]
    psum x1 -> x0, blocking collectives: 45 us -> none  [shards(): adapter_load = lax.psum(tallies, 'ba')]
    unnamed x13 -> x22, local copies, waits for them, and re-layouts: 0.59 us -> 10.8 us
    all_to_all x1 -> x0, starting transfers between devices: 6.05 us -> none  [shards(): lax.all_to_all(reduced, 'ba', split_axis=0, concat_axis=0, tiled=True)]
    dot_general x7 -> x3, matrix products: 64.3 us -> 59.8 us  [the longest x1 23.5 us: shards(): gate_proj = jnp.dot(rows, gate_weight[0], preferred_element_type=F32)]
  transfers between devices with their start and end apart: 3 -> 0, of which waited for: 2 -> 0; matrix products, arithmetic and copies ran while one was open for 1% -> 0% of each run, Pallas kernels for 0% -> 0%
where the time goes in v1:
time: 161 us; the launch traced here: 159 us
  Pallas kernels  86 us (53%)
  matrix products  59.8 us (37%)
  local copies, waits for them, and re-layouts  11.4 us (7%)
    pallas_call x1, Pallas kernels, shards(): pl.pallas_call(functools.partial(front, n_aa, n_ba, model_width), out_sha...  51.5 us
    pallas_call x1, Pallas kernels, shards(): pl.pallas_call(functools.partial(back, n_aa, n_ba), out_shape=jax.ShapeDt...  34.5 us
    dot_general x1, matrix products, shards(): gate_proj = jnp.dot(rows, gate_weight[0], preferred_element_type=F32)  23.5 us
    dot_general x1, matrix products, shards(): jnp.dot(hidden, down_weight[0], preferred_element_type=F32).astype(BF16)  18.2 us
    dot_general x1, matrix products, shards(): up_proj = jnp.dot(rows, up_weight[0], preferred_element_type=F32)  18 us
    unnamed x22, local copies, waits for them, and re-layouts  10.8 us

profile of v1, /device:TPU:8, one launch (start us, length us, event | category | flops | bytes accessed | tf_op | source)
XLA Modules:
  0.0 158.6 jit_solution(10115536351519696991)
XLA Ops:
  0.6 0.7 pad_add_fusion
  1.3 0.1 copy.18.idx_ref
  1.4 0.0 copy-start.4
  1.5 1.3 copy.17.router_ref
  2.8 0.0 copy-start
  2.8 1.2 copy-done
  4.0 0.0 copy-start.1
  4.0 1.2 copy-done.1
  5.3 0.0 copy-start.2
  5.3 1.2 copy-done.2
  6.5 0.0 copy-start.3
  6.5 1.2 copy-done.3
  7.7 0.0 copy-start.7
  7.7 0.7 copy-done.7
  8.4 0.0 copy-start.8
  8.4 0.7 copy-done.8
  9.1 51.5 %front.1 = (bf16[8,48,4096]{2,1,0:T(8,128)(2,1)}, f32[128,1024]{1,0:T(8,128)S(1)}, f32[128,8]{1,0:T(8,128)S(1)}, f32[8,128]{1,0:T(8,128)S(1)}) custom-call(s32[128,3]{1,0:T(8,128)S(1)} %copy.18.idx_ref, s32[2,128]{1,0:T(2,128)S(1)} %bitcast.35, bf16[128,4096]{1,0:T(8,128)(2,1)S(1)} %copy-done, bf16[128,4096]{1,0:T(8,128)(2,1)S(1)} %copy-done.1, ...), custom_call_target="tpu_custom_call" | custom-call | tf_op jit(solution)/shard_map/front/pallas_call | solution.py:298
  60.6 0.0 copy-start.5
  60.6 0.8 copy-done.5
  61.4 0.0 copy-start.6
  61.4 0.6 copy-done.6
  62.1 0.5 slice_bitcast_fusion
  62.6 0.0 copy-start.9
  62.6 23.5 %fusion.4 = f32[384,3584]{1,0:T(8,128)} fusion(bf16[384,4096]{1,0:T(8,128)(2,1)} %bitcast.38, bf16[1,4096,3584]{2,1,0:T(8,128)(2,1)} %param.19), kind=kOutput, calls=%fused_computation.4 | convolution fusion | flops 11274289152 | bytes 38010880 | tf_op jit(solution)/shard_map/dot_general | solution.py:330
  86.1 0.0 copy-done.4
  86.1 0.0 copy-done.9
  86.1 18.0 %fusion.12.clone.4 = bf16[384,3584]{1,0:T(8,128)(2,1)S(1)} fusion(bf16[384,4096]{1,0:T(8,128)(2,1)S(1)} %bitcast.39, bf16[1,4096,3584]{2,1,0:T(8,128)(2,1)} %param.20, f32[384,3584]{1,0:T(8,128)} %fusion.4), kind=kOutput, calls=%fused_computation.8.clone.clone.clone.1 | convolution fusion | flops 11282546688 | bytes 40763392 | tf_op jit(solution)/shard_map/dot_general | solution.py:331
  104.2 18.2 %fusion.9 = bf16[384,4096]{1,0:T(8,128)(2,1)} fusion(bf16[1,3584,4096]{2,1,0:T(8,128)(2,1)} %param.21, bf16[384,3584]{1,0:T(8,128)(2,1)S(1)} %fusion.12.clone.4), kind=kOutput, calls=%fused_computation.7 | convolution fusion | flops 11275862016 | bytes 35258368 | tf_op jit(solution)/shard_map/dot_general | solution.py:333
  122.4 34.5 %back.1 = bf16[128,1024]{1,0:T(8,128)(2,1)} custom-call(s32[128,3]{1,0:T(8,128)} %copy-done.4, f32[128,1024]{1,0:T(8,128)} %copy-done.5, f32[128,8]{1,0:T(8,128)} %copy-done.6, bf16[8,48,4096]{2,1,0:T(8,128)(2,1)} %bitcast.36), custom_call_target="tpu_custom_call" | custom-call | tf_op jit(solution)/shard_map/back/pallas_call | solution.py:334
  157.0 1.7 %copy.20 = bf16[128,1024]{1,0:T(8,128)(2,1)} copy(bf16[128,1024]{1,0:T(8,128)(2,1)} %back.1) | data formatting | bytes 524288
Async XLA Ops:
  1.4 84.7 %copy-start.4 = (s32[128,3]{1,0:T(8,128)}, s32[128,3]{1,0:T(8,128)S(1)}, u32[]{:S(2)}) copy-start(s32[128,3]{1,0:T(8,128)S(1)} %copy.18.idx_ref) | copy-start | bytes 4612
  2.8 1.2 copy-start
  4.0 1.2 copy-start.1
  5.3 1.2 copy-start.2
  6.5 1.2 copy-start.3
  7.7 0.7 copy-start.7
  8.4 0.7 copy-start.8
  60.6 0.9 copy-start.5
  61.4 0.6 copy-start.6
  62.6 23.5 %copy-start.9 = (bf16[8,48,4096]{2,1,0:T(8,128)(2,1)S(1)}, bf16[8,48,4096]{2,1,0:T(8,128)(2,1)}, u32[]{:S(2)}) copy-start(bf16[8,48,4096]{2,1,0:T(8,128)(2,1)} %get-tuple-element.8) | copy-start | bytes 9437188
